TPU v7x, 32 devices: a whole 2x2x4 slice. The times are simulated.
32 devices in a mesh: emit: 2 (over y), client: 16 (over z, x, core).
Axes of the slice: x: 2, y: 2, z: 4, core: 2. Of those that a mesh axis runs over, the one named last changes fastest.
Arguments:
- features: bfloat16 [65536, 768], P('client'), may hold values from -28 to 28
- labels: int32 [65536], P('client'), may hold values from 0 to 999
- client_ids: int32 [128], replicated, may hold values from 0 to 127, each once
- trunk_in: bfloat16 [128, 2048], replicated, may hold values from -6 to 6
- trunk_weight: bfloat16 [2048, 2048], P(None, 'client'), may hold values from -0.125 to 0.125
- class_table: bfloat16 [1000, 2048], P('emit'), may hold values from -6 to 6
- emit_weight: bfloat16 [2048, 768], P('emit'), may hold values from -0.125 to 0.125
Outputs:
- loss: float32 [65536], P('client')
- emit_grad: float32 [2048, 768], P(('emit', 'client'))
- trunk_grad: float32 [2048, 2048], P(None, ('emit', 'client'))
Inputs may be any that keep to these rules, and one draw needn't show every extreme that they name: Each client number appears once; slot s holds the features of client client_ids[s].
All inputs are finite; a program needn't handle non-finite values.
Results may differ from a plain program's by a relative error of at most 0.022.
Values may be sent and summed in bfloat16 or wider, within the bound.
No kernel may reach another device: no remote copies, remote signals or barrier semaphores. Data moves between devices by JAX's collectives and lax.ppermute only.
A program may use at most 128 MiB of HBM per device.

v0:
```python
import jax
import jax.numpy as jnp
from jax import lax
from jax.sharding import PartitionSpec as P

CL_DEV = 8


def silu_grad(value):
    sig = jax.nn.sigmoid(value)
    return sig * (1.0 + value * (1.0 - sig))


def per_device(features, labels, client_ids, trunk_in, trunk_weight, class_table, emit_weight):
    slots = CL_DEV
    clients = trunk_in.shape[0]
    hidden_dim = trunk_in.shape[1]
    classes = class_table.shape[0]
    feat_dim = features.shape[1]
    samples = features.shape[0] // slots
    client_index = lax.axis_index("client")
    emit_index = lax.axis_index("emit")
    pre_cols = jnp.dot(trunk_in, trunk_weight, preferred_element_type=jnp.float32).astype(
        jnp.bfloat16
    )
    pre_all = lax.all_gather(pre_cols, "client", axis=1, tiled=True)
    own_ids = lax.dynamic_slice_in_dim(client_ids, client_index * slots, slots)
    numbers = lax.iota(jnp.int32, clients)
    picker = (own_ids[:, None] == numbers[None, :]).astype(jnp.bfloat16)
    pre_own = jnp.dot(picker, pre_all, preferred_element_type=jnp.float32)
    code_in = jax.nn.silu(pre_own)[:, None, :] + class_table.astype(jnp.float32)[None, :, :]
    code = jax.nn.silu(code_in).astype(jnp.bfloat16).reshape(slots * classes, hidden_dim)
    emit_full = lax.all_gather(emit_weight, "emit", axis=0, tiled=True)
    heads = jnp.dot(code, emit_full, preferred_element_type=jnp.float32).astype(jnp.bfloat16)
    heads = heads.reshape(slots, classes, feat_dim)
    feats = features.reshape(slots, samples, feat_dim)
    logits = jnp.einsum("snd,skd->snk", feats, heads, preferred_element_type=jnp.float32)
    class_ids = emit_index * classes + lax.iota(jnp.int32, classes)
    onehot = (labels.reshape(slots, samples)[:, :, None] == class_ids[None, None, :]).astype(
        jnp.float32
    )
    target = jnp.sum(logits * onehot, axis=2)
    local_top = jnp.max(logits, axis=2)
    top = lax.pmax(local_top, "emit")
    expd = jnp.exp(logits - top[:, :, None])
    total, target_all = (
        lax.psum(jnp.sum(expd, axis=2).astype(jnp.bfloat16), "emit").astype(jnp.float32),
        lax.psum(target.astype(jnp.bfloat16), "emit").astype(jnp.float32),
    )
    loss = (top + jnp.log(total) - target_all).reshape(slots * samples)
    grad_logits = ((expd / total[:, :, None] - onehot) / clients).astype(jnp.bfloat16)
    grad_heads = jnp.einsum("snk,snd->skd", grad_logits, feats, preferred_element_type=jnp.float32)
    grad_heads = grad_heads.astype(jnp.bfloat16).reshape(slots * classes, feat_dim)
    partial_rows = lax.psum_scatter(
        jnp.einsum("rh,rd->hd", code, grad_heads, preferred_element_type=jnp.float32).astype(
            jnp.bfloat16
        ),
        "emit",
        scatter_dimension=0,
        tiled=True,
    )
    emit_grad = lax.psum_scatter(partial_rows, "client", scatter_dimension=0, tiled=True).astype(
        jnp.float32
    )
    grad_code = jnp.dot(grad_heads, emit_full.T, preferred_element_type=jnp.float32)
    grad_code = grad_code.reshape(slots, classes, hidden_dim)
    grad_sum = jnp.sum(grad_code * silu_grad(code_in), axis=1)
    block = hidden_dim // lax.axis_size("emit")
    grad_block = lax.psum_scatter(
        grad_sum.astype(jnp.bfloat16), "emit", scatter_dimension=1, tiled=True
    ).astype(jnp.float32)
    pre_block = lax.dynamic_slice_in_dim(pre_own, emit_index * block, block, 1)
    grad_pre = (grad_block * silu_grad(pre_block)).astype(jnp.bfloat16)
    grad_all = lax.all_gather(grad_pre, "client", axis=0, tiled=True)
    width = block // lax.axis_size("client")
    grad_mine = lax.dynamic_slice_in_dim(grad_all, client_index * width, width, 1)
    picker_all = (client_ids[:, None] == numbers[None, :]).astype(jnp.bfloat16)
    grad_client = jnp.einsum(
        "sc,sw->cw", picker_all, grad_mine, preferred_element_type=jnp.float32
    ).astype(jnp.bfloat16)
    trunk_grad = jnp.einsum("ch,cw->hw", trunk_in, grad_client, preferred_element_type=jnp.float32)
    return (loss, emit_grad, trunk_grad)


def solution(mesh):
    return jax.shard_map(
        per_device,
        mesh=mesh,
        in_specs=(
            P("client", None),
            P("client"),
            P(),
            P(),
            P(None, "client"),
            P("emit", None),
            P("emit", None),
        ),
        out_specs=(P("client"), P(("emit", "client"), None), P(None, ("emit", "client"))),
        check_vma=False,
    )
```

profile of v0, /device:TPU:0, one launch (start us, length us, event | category | flops | bytes accessed | tf_op | source)
XLA Modules:
  0.0 301.0 jit_solution(15818444923644420480)
XLA Ops:
  7.2 0.0 copy-start
  7.2 0.0 all-gather.2.cloned.1.call-start
  7.2 0.7 all-gather.2.cloned.1.call-update
  7.9 0.0 reduce-scatter.4.cloned.1.call-start
  8.0 4.1 %convert_element_type.57 = f32[500,2048]{1,0:T(8,128)} convert(bf16[500,2048]{1,0:T(8,128)(2,1)} %param.12) | non-fusion elementwise | flops 1024000 | bytes 6144000 | tf_op jit(solution)/shard_map/convert_element_type | solution.py:31
  12.1 0.7 dynamic_slice.9
  12.8 0.0 copy-done
  12.8 1.3 convolution_convert_fusion.1
  14.1 24.6 %all_gather.9 = bf16[128,2048]{1,0:T(8,128)(2,1)S(1)} all-gather(bf16[128,128]{1,0:T(8,128)(2,1)S(1)} %convolution_convert_fusion.1), channel_id=1, replica_groups=mesh['emit'=2,'client'=16] {'client'}, dimensions={1}, use_global_device_ids=true | all-gather | bytes 557056 | tf_op jit(solution)/shard_map/all_gather | solution.py:26
  38.7 0.9 divide_multiply_fusion
  39.6 12.5 %broadcast_add_fusion = f32[8,500,2048]{2,1,0:T(8,128)} fusion(f32[500,2048]{1,0:T(8,128)} %convert_element_type.57, f32[8,2048]{1,0:T(8,128)S(1)} %get-tuple-element.7), kind=kLoop, calls=%fused_computation.15 | loop fusion | flops 8192000 | bytes 36929536 | tf_op jit(solution)/shard_map/add | solution.py:31
  52.1 0.0 copy-start.3
  52.1 29.4 %add.75 = f32[4000,2048]{1,0:T(8,128)} reshape(f32[8,500,2048]{2,1,0:T(8,128)} %broadcast_add_fusion) | data formatting | bytes 65536000 | tf_op jit(solution)/shard_map/add | solution.py:31
  81.5 0.0 copy-done.3
  81.5 0.0 all-gather.2.cloned.1.call-done
  81.5 25.7 %fusion.20 = bf16[4000,768]{1,0:T(8,128)(2,1)} fusion(bf16[2048,768]{1,0:T(8,128)(2,1)} %all-gather.2.cloned.1.call-done, f32[4000,2048]{1,0:T(8,128)} %add.75), kind=kOutput, calls=%fused_computation.28 | convolution fusion | flops 12626944000 | bytes 42057728 | tf_op jit(solution)/shard_map/dot_general | solution.py:34
  107.2 6.3 %reshape.34 = bf16[8,500,768]{2,1,0:T(8,128)(2,1)} reshape(bf16[4000,768]{1,0:T(8,128)(2,1)} %fusion.20) | data formatting | bytes 12288000 | tf_op jit(solution)/shard_map/reshape | solution.py:35
  113.5 11.2 %bitcast_reduce_fusion = (f32[8,512]{1,0:T(8,128)S(1)}, f32[8,500,512]{2,1,0:T(8,128)}) fusion(bf16[8,500,768]{2,1,0:T(8,128)(2,1)} %reshape.34, bf16[8,512,768]{2,1,0:T(8,128)(2,1)} %bitcast.35), kind=kOutput, calls=%fused_computation.25 | convolution fusion | flops 3147771904 | bytes 20643840 | tf_op jit(solution)/shard_map/snd,skd->snk/dot_general | solution.py:37
  124.7 8.2 %pmax.7 = f32[8,512]{1,0:T(8,128)S(1)} all-reduce(f32[8,512]{1,0:T(8,128)S(1)} %get-tuple-element.9), channel_id=1, replica_groups=mesh['emit'=2,'client'=16] {'emit'}, use_global_device_ids=true, to_apply=%region_1.2 | all-reduce | flops 4096 | bytes 32768 | tf_op jit(solution)/shard_map/pmax | solution.py:44
  132.8 4.5 %fusion.19 = (bf16[8,512]{1,0:T(8,128)(2,1)S(1)}, bf16[8,512]{1,0:T(8,128)(2,1)S(1)}) fusion(f32[8,500,512]{2,1,0:T(8,128)} %get-tuple-element.10, f32[8,512]{1,0:T(8,128)S(1)} %pmax.7, s32[500]{0:T(512)S(1)} %iota_add_fusion, s32[8,512]{1,0:T(8,128)S(1)} %eq.44), kind=kLoop, calls=%fused_computation.27 | loop fusion | flops 10231808 | bytes 8243152 | tf_op jit(solution)/shard_map/reduce_sum | solution.py:47
  137.4 7.1 %all-reduce = (bf16[8,512]{1,0:T(8,128)(2,1)S(1)}, bf16[8,512]{1,0:T(8,128)(2,1)S(1)}) all-reduce(bf16[8,512]{1,0:T(8,128)(2,1)S(1)} %get-tuple-element.4, bf16[8,512]{1,0:T(8,128)(2,1)S(1)} %get-tuple-element.3), channel_id=1, replica_groups=mesh['emit'=2,'client'=16] {'emit'}, use_global_device_ids=true, to_apply=%region_5.6 | all-reduce | flops 8192 | bytes 32768 | tf_op jit(solution)/shard_map/psum | solution.py:48
  144.5 0.0 copy-start.1
  144.5 11.5 %fusion.30 = bf16[8,500,768]{2,1,0:T(8,128)(2,1)} fusion(bf16[8,512,768]{2,1,0:T(8,128)(2,1)} %bitcast.36, f32[8,500,512]{2,1,0:T(8,128)} %get-tuple-element.10, f32[8,512]{1,0:T(8,128)S(1)} %convert_element_type.61, s32[8,512]{1,0:T(8,128)S(1)} %eq.44, f32[8,512]{1,0:T(8,128)S(1)} %pmax.7, s32[500]{0:T(512)S(1)} %iota_add_fusion), kind=kOutput, calls=%fused_computation.36 | convolution fusion | flops 3163136000 | bytes 20678608 | tf_op jit(solution)/shard_map/snk,snd->skd/dot_general | solution.py:52
  156.0 0.0 copy-done.1
  156.0 20.2 %bitcast_convert_fusion = bf16[2048,768]{1,0:T(8,128)(2,1)} fusion(bf16[8,500,768]{2,1,0:T(8,128)(2,1)} %fusion.30, f32[500,2048]{1,0:T(8,128)S(1)} %copy-done.1, f32[8,2048]{1,0:T(8,128)S(1)} %get-tuple-element.7), kind=kOutput, calls=%fused_computation.29 | convolution fusion | flops 12633636864 | bytes 13451264 | tf_op jit(solution)/shard_map/rh,rd->hd/dot_general | solution.py:55
  176.2 0.0 reduce-scatter.4.cloned.1.call-update
  176.2 0.0 copy-start.2
  176.2 0.0 copy-start.4
  176.2 0.0 reduce-scatter.8.cloned.1.call-start
  176.3 24.4 %fusion.7 = bf16[8,2048]{1,0:T(8,128)(2,1)} fusion(bf16[8,500,768]{2,1,0:T(8,128)(2,1)} %fusion.30, f32[500,2048]{1,0:T(8,128)} %convert_element_type.57, f32[8,2048]{1,0:T(8,128)S(1)} %get-tuple-element.7, bf16[2048,768]{1,0:T(8,128)(2,1)} %all-gather.2.cloned.1.call-done), kind=kOutput, calls=%fused_computation.10 | convolution fusion | flops 12664815616 | bytes 13484032 | tf_op jit(solution)/shard_map/dot_general | solution.py:65
  200.7 0.0 reduce-scatter.8.cloned.1.call-update
  200.7 0.0 reduce-scatter.6.cloned.1.call-start
  200.8 16.3 %reduce-scatter.4.cloned.1.call-done = bf16[1024,768]{1,0:T(8,128)(2,1)} async-done(((bf16[2048,768]{1,0:T(8,128)(2,1)}), bf16[1024,768]{1,0:T(8,128)(2,1)}) %reduce-scatter.4.cloned.1.call-update) | async-done | bytes 1572880 | tf_op jit(solution)/shard_map/reduce_scatter | solution.py:54
  217.1 0.0 reduce-scatter.6.cloned.1.call-update
  217.1 0.6 copy.10
  217.7 12.1 %reduce-scatter.8.cloned.1.call-done = bf16[8,1024]{1,0:T(8,128)(2,1)} async-done(((bf16[8,2048]{1,0:T(8,128)(2,1)}), bf16[8,1024]{1,0:T(8,128)(2,1)}) %reduce-scatter.8.cloned.1.call-update) | async-done | bytes 16400 | tf_op jit(solution)/shard_map/reduce_scatter | solution.py:69
  229.8 0.0 copy-done.2
  229.8 0.7 multiply_convert_fusion.4
  230.6 22.0 %all_gather.11 = bf16[128,1024]{1,0:T(8,128)(2,1)S(1)} all-gather(bf16[8,1024]{1,0:T(8,128)(2,1)S(1)} %multiply_convert_fusion.4), channel_id=1, replica_groups=mesh['emit'=2,'client'=16] {'client'}, dimensions={0}, use_global_device_ids=true | all-gather | bytes 278528 | tf_op jit(solution)/shard_map/all_gather | solution.py:74
  252.6 0.0 copy-done.4
  252.6 1.3 convolution_bitcast_fusion
  253.9 39.0 %reduce-scatter.6.cloned.1.call-done = bf16[64,768]{1,0:T(8,128)(2,1)} async-done(((bf16[1024,768]{1,0:T(8,128)(2,1)}), bf16[64,768]{1,0:T(8,128)(2,1)}) %reduce-scatter.6.cloned.1.call-update) | async-done | bytes 98320 | tf_op jit(solution)/shard_map/reduce_scatter | solution.py:62
  292.9 1.6 convert_element_type.69
  (4 shorter events, 0.0 us)
Async XLA Ops:
  7.2 5.6 %copy-start = (bf16[128,2048]{1,0:T(8,128)(2,1)S(1)}, bf16[128,2048]{1,0:T(8,128)(2,1)}, u32[]{:S(2)}) copy-start(bf16[128,2048]{1,0:T(8,128)(2,1)} %param.10) | copy-start | bytes 1572868
  7.2 74.3 %all-gather.2.cloned.1.call-start = ((), (), s32[]{:S(2)}) async-start(), calls=%async_computation.3 | async-start | bytes 4718592 | tf_op jit(solution)/shard_map/all_gather | solution.py:33
  7.9 209.2 %reduce-scatter.4.cloned.1.call-start = ((), (), s32[]{:S(2)}) async-start(), calls=%async_computation.4 | async-start | bytes 4718592 | tf_op jit(solution)/shard_map/reduce_scatter | solution.py:54
  52.1 29.4 %copy-start.3 = (s32[4096]{0:T(1024)S(1)}, s32[4096]{0:T(1024)}, u32[]{:S(2)}) copy-start(s32[4096]{0:T(1024)} %param.8) | copy-start | bytes 49156
  144.5 11.5 %copy-start.1 = (f32[500,2048]{1,0:T(8,128)S(1)}, f32[500,2048]{1,0:T(8,128)}, u32[]{:S(2)}) copy-start(f32[500,2048]{1,0:T(8,128)} %convert_element_type.57) | copy-start | bytes 12288004
  176.2 53.6 %copy-start.2 = (f32[8,2048]{1,0:T(8,128)S(1)}, f32[8,2048]{1,0:T(8,128)}, u32[]{:S(2)}) copy-start(f32[8,2048]{1,0:T(8,128)} %get-tuple-element.8) | copy-start | bytes 196612
  176.2 76.4 %copy-start.4 = (s32[128]{0:T(128)S(1)}, s32[128]{0:T(128)}, u32[]{:S(2)}) copy-start(s32[128]{0:T(128)} %param.9) | copy-start | bytes 1540
  176.2 53.6 %reduce-scatter.8.cloned.1.call-start = ((), (), s32[]{:S(2)}) async-start(), calls=%async_computation.6 | async-start | bytes 49152 | tf_op jit(solution)/shard_map/reduce_scatter | solution.py:69
  200.7 92.2 %reduce-scatter.6.cloned.1.call-start = ((), (), s32[]{:S(2)}) async-start(), calls=%async_computation.5 | async-start | bytes 1671168 | tf_op jit(solution)/shard_map/reduce_scatter | solution.py:62
Sparse Core Ops, SparseCore 0:
  9.5 47.6 all-gather.1
  176.3 40.7 reduce-scatter.3
  219.8 9.9 reduce-scatter.7
  233.3 59.5 reduce-scatter.5
where the time goes:
time: 302 us; the launch traced here: 301 us
  matrix products  96.5 us (32%)
  waiting for transfers between devices  68.1 us (23%)
  blocking collectives  61.9 us (20%)
  local copies, waits for them, and re-layouts  37.1 us (12%)
  other arithmetic  23.4 us (8%)
  between operations  13.8 us (5%)
    reduce_scatter x1, waiting for transfers between devices, per_device(): lax.psum_scatter(partial_rows, 'client', scatter_dimension=0, tiled=True)  39 us
    add x1, local copies, waits for them, and re-layouts, per_device(): jax.nn.silu(pre_own)[:, None, :]  29.4 us
    dot_general x1, matrix products, per_device(): jnp.dot(code, emit_full, preferred_element_type=jnp.float32)  25.7 us
    all_gather x1, blocking collectives, per_device(): pre_all = lax.all_gather(pre_cols, 'client', axis=1, tiled=True)  24.6 us
    dot_general x1, matrix products, per_device(): jnp.dot(grad_heads, emit_full.T, preferred_element_type=jnp.float32)  24.4 us
    all_gather x1, blocking collectives, per_device(): grad_all = lax.all_gather(grad_pre, 'client', axis=0, tiled=True)  22 us
    dot_general x1, matrix products, per_device(): jnp.einsum('rh,rd->hd', code, grad_heads, preferred_element_type=jnp.floa...  20.2 us
    reduce_scatter x1, waiting for transfers between devices, per_device(): lax.psum_scatter(jnp.einsum('rh,rd->hd', code, grad_heads, preferred_elem...  16.3 us
  transfers between devices with their start and end apart: 4, of which 3 were waited for; matrix products, arithmetic and copies ran while one was open for 25% of the time, Pallas kernels for 0%

commit v1 on v0

--- a/solution.py
+++ b/solution.py
@@ -71,7 +71,14 @@
     ).astype(jnp.float32)
     pre_block = lax.dynamic_slice_in_dim(pre_own, emit_index * block, block, 1)
     grad_pre = (grad_block * silu_grad(pre_block)).astype(jnp.bfloat16)
-    grad_all = lax.all_gather(grad_pre, "client", axis=0, tiled=True)
+    ring = [grad_pre]
+    for hop in range(15):
+        ring.append(lax.ppermute(ring[-1], "client", [(dev, (dev + 1) % 16) for dev in range(16)]))
+    grad_all = jnp.roll(
+        jnp.concatenate(ring[::-1], axis=0),
+        (lax.axis_index("client") + 1) * ring[0].shape[0],
+        axis=0,
+    )
     width = block // lax.axis_size("client")
     grad_mine = lax.dynamic_slice_in_dim(grad_all, client_index * width, width, 1)
     picker_all = (client_ids[:, None] == numbers[None, :]).astype(jnp.bfloat16)

time: 302 us -> 356 us (1.18)
  waiting for transfers between devices: 68.1 us -> 143 us
  blocking collectives: 61.9 us -> 39.9 us
    ppermute x0 -> x15, waiting for transfers between devices: none -> 87.2 us  [per_device(): lax.ppermute(ring[-1], 'client', [(dev, (dev + 1) % 16) for dev in range(...]
    all_gather x1 -> x0, blocking collectives: 22 us -> none  [per_device(): grad_all = lax.all_gather(grad_pre, 'client', axis=0, tiled=True)]
    reduce_scatter x1, waiting for transfers between devices: 39 us -> 55.4 us  [per_device(): lax.psum_scatter(partial_rows, 'client', scatter_dimension=0, tiled=True)]
    reduce_scatter x1, waiting for transfers between devices: 16.3 us -> 0.02 us  [per_device(): lax.psum_scatter(jnp.einsum('rh,rd->hd', code, grad_heads, preferred_elem...]
    reduce_scatter x1, waiting for transfers between devices: 12.1 us -> 0.02 us  [per_device(): lax.psum_scatter(grad_sum.astype(jnp.bfloat16), 'emit', scatter_dimension...]
  transfers between devices with their start and end apart: 4 -> 19, of which waited for: 3 -> 16; matrix products, arithmetic and copies ran while one was open for 25% -> 20% of each run, Pallas kernels for 0% -> 0%
where the time goes in v1:
time: 356 us; the launch traced here: 355 us
  waiting for transfers between devices  143 us (40%)
  matrix products  97 us (27%)
  blocking collectives  39.9 us (11%)
  local copies, waits for them, and re-layouts  37.1 us (10%)
  other arithmetic  23.4 us (7%)
  between operations  14.1 us (4%)
    ppermute x15, waiting for transfers between devices, per_device(): lax.ppermute(ring[-1], 'client', [(dev, (dev + 1) % 16) for dev in range(...  87.2 us
    reduce_scatter x1, waiting for transfers between devices, per_device(): lax.psum_scatter(partial_rows, 'client', scatter_dimension=0, tiled=True)  55.4 us
    add x1, local copies, waits for them, and re-layouts, per_device(): jax.nn.silu(pre_own)[:, None, :]  29.3 us
    dot_general x1, matrix products, per_device(): jnp.dot(code, emit_full, preferred_element_type=jnp.float32)  25.7 us
    dot_general x1, matrix products, per_device(): jnp.dot(grad_heads, emit_full.T, preferred_element_type=jnp.float32)  24.6 us
    all_gather x1, blocking collectives, per_device(): pre_all = lax.all_gather(pre_cols, 'client', axis=1, tiled=True)  24.6 us
    dot_general x1, matrix products, per_device(): jnp.einsum('rh,rd->hd', code, grad_heads, preferred_element_type=jnp.floa...  20.5 us
    add x1, other arithmetic, per_device(): jax.nn.silu(pre_own)[:, None, :]  12.5 us
  transfers between devices with their start and end apart: 19, of which 16 were waited for; matrix products, arithmetic and copies ran while one was open for 20% of the time, Pallas kernels for 0%

profile of v1, /device:TPU:0, one launch (start us, length us, event | category | flops | bytes accessed | tf_op | source)
XLA Modules:
  0.0 355.1 jit_solution(14560624058617870971)
XLA Ops:
  7.2 0.0 copy-start
  7.2 0.0 all-gather.2.cloned.1.call-start
  7.2 0.7 all-gather.2.cloned.1.call-update
  7.9 0.0 reduce-scatter.8.cloned.1.call-start
  8.0 4.1 %convert_element_type.57 = f32[500,2048]{1,0:T(8,128)} convert(bf16[500,2048]{1,0:T(8,128)(2,1)} %param.12) | non-fusion elementwise | flops 1024000 | bytes 6144000 | tf_op jit(solution)/shard_map/convert_element_type | solution.py:31
  12.0 0.7 dynamic_slice.11
  12.8 1.3 convolution_convert_fusion.1
  14.1 24.6 %all_gather.6 = bf16[128,2048]{1,0:T(8,128)(2,1)S(1)} all-gather(bf16[128,128]{1,0:T(8,128)(2,1)S(1)} %convolution_convert_fusion.1), channel_id=1, replica_groups=mesh['emit'=2,'client'=16] {'client'}, dimensions={1}, use_global_device_ids=true | all-gather | bytes 557056 | tf_op jit(solution)/shard_map/all_gather | solution.py:26
  38.7 0.9 divide_multiply_fusion
  39.6 12.5 %broadcast_add_fusion = f32[8,500,2048]{2,1,0:T(8,128)} fusion(f32[500,2048]{1,0:T(8,128)} %convert_element_type.57, f32[8,2048]{1,0:T(8,128)S(1)} %get-tuple-element.7), kind=kLoop, calls=%fused_computation.15 | loop fusion | flops 8192000 | bytes 36929536 | tf_op jit(solution)/shard_map/add | solution.py:31
  52.0 29.3 %add.90 = f32[4000,2048]{1,0:T(8,128)} reshape(f32[8,500,2048]{2,1,0:T(8,128)} %broadcast_add_fusion) | data formatting | bytes 65536000 | tf_op jit(solution)/shard_map/add | solution.py:31
  81.4 0.0 all-gather.2.cloned.1.call-done
  81.4 25.7 %fusion.20 = bf16[4000,768]{1,0:T(8,128)(2,1)} fusion(bf16[2048,768]{1,0:T(8,128)(2,1)} %all-gather.2.cloned.1.call-done, f32[4000,2048]{1,0:T(8,128)} %add.90), kind=kOutput, calls=%fused_computation.28 | convolution fusion | flops 12626944000 | bytes 42057728 | tf_op jit(solution)/shard_map/dot_general | solution.py:34
  107.1 6.3 %reshape.34 = bf16[8,500,768]{2,1,0:T(8,128)(2,1)} reshape(bf16[4000,768]{1,0:T(8,128)(2,1)} %fusion.20) | data formatting | bytes 12288000 | tf_op jit(solution)/shard_map/reshape | solution.py:35
  113.4 11.2 %bitcast_reduce_fusion = (f32[8,512]{1,0:T(8,128)S(1)}, f32[8,500,512]{2,1,0:T(8,128)}) fusion(bf16[8,500,768]{2,1,0:T(8,128)(2,1)} %reshape.34, bf16[8,512,768]{2,1,0:T(8,128)(2,1)} %bitcast.35), kind=kOutput, calls=%fused_computation.25 | convolution fusion | flops 3147771904 | bytes 20643840 | tf_op jit(solution)/shard_map/snd,skd->snk/dot_general | solution.py:37
  124.5 8.2 %pmax.7 = f32[8,512]{1,0:T(8,128)S(1)} all-reduce(f32[8,512]{1,0:T(8,128)S(1)} %get-tuple-element.9), channel_id=1, replica_groups=mesh['emit'=2,'client'=16] {'emit'}, use_global_device_ids=true, to_apply=%region_1.2 | all-reduce | flops 4096 | bytes 32768 | tf_op jit(solution)/shard_map/pmax | solution.py:44
  132.7 4.5 %fusion.19 = (bf16[8,512]{1,0:T(8,128)(2,1)S(1)}, bf16[8,512]{1,0:T(8,128)(2,1)S(1)}) fusion(f32[8,500,512]{2,1,0:T(8,128)} %get-tuple-element.10, f32[8,512]{1,0:T(8,128)S(1)} %pmax.7, s32[500]{0:T(512)S(1)} %iota_add_fusion, s32[8,512]{1,0:T(8,128)S(1)} %eq.47), kind=kLoop, calls=%fused_computation.27 | loop fusion | flops 10231808 | bytes 8243152 | tf_op jit(solution)/shard_map/reduce_sum | solution.py:47
  137.3 7.1 %all-reduce = (bf16[8,512]{1,0:T(8,128)(2,1)S(1)}, bf16[8,512]{1,0:T(8,128)(2,1)S(1)}) all-reduce(bf16[8,512]{1,0:T(8,128)(2,1)S(1)} %get-tuple-element.4, bf16[8,512]{1,0:T(8,128)(2,1)S(1)} %get-tuple-element.3), channel_id=1, replica_groups=mesh['emit'=2,'client'=16] {'emit'}, use_global_device_ids=true, to_apply=%region_5.6 | all-reduce | flops 8192 | bytes 32768 | tf_op jit(solution)/shard_map/psum | solution.py:48
  144.4 11.5 %fusion.30 = bf16[8,500,768]{2,1,0:T(8,128)(2,1)} fusion(bf16[8,512,768]{2,1,0:T(8,128)(2,1)} %bitcast.36, f32[8,500,512]{2,1,0:T(8,128)} %get-tuple-element.10, f32[8,512]{1,0:T(8,128)S(1)} %convert_element_type.61, s32[8,512]{1,0:T(8,128)S(1)} %eq.47, f32[8,512]{1,0:T(8,128)S(1)} %pmax.7, s32[500]{0:T(512)S(1)} %iota_add_fusion), kind=kOutput, calls=%fused_computation.36 | convolution fusion | flops 3163136000 | bytes 20678608 | tf_op jit(solution)/shard_map/snk,snd->skd/dot_general | solution.py:52
  155.8 24.6 %fusion.7 = bf16[8,2048]{1,0:T(8,128)(2,1)} fusion(bf16[8,500,768]{2,1,0:T(8,128)(2,1)} %fusion.30, f32[500,2048]{1,0:T(8,128)S(1)} %copy-done.1, f32[8,2048]{1,0:T(8,128)S(1)} %get-tuple-element.7, bf16[2048,768]{1,0:T(8,128)(2,1)} %all-gather.2.cloned.1.call-done), kind=kOutput, calls=%fused_computation.10 | convolution fusion | flops 12664815616 | bytes 13484032 | tf_op jit(solution)/shard_map/dot_general | solution.py:65
  180.4 0.0 reduce-scatter.8.cloned.1.call-update
  180.5 0.0 copy-start.2
  180.5 0.0 copy-start.4
  180.5 0.0 reduce-scatter.4.cloned.1.call-start
  180.5 20.5 %bitcast_convert_fusion = bf16[2048,768]{1,0:T(8,128)(2,1)} fusion(bf16[8,500,768]{2,1,0:T(8,128)(2,1)} %fusion.30, f32[500,2048]{1,0:T(8,128)} %convert_element_type.57, f32[8,2048]{1,0:T(8,128)S(1)} %get-tuple-element.7), kind=kOutput, calls=%fused_computation.29 | convolution fusion | flops 12633636864 | bytes 13451264 | tf_op jit(solution)/shard_map/rh,rd->hd/dot_general | solution.py:55
  201.1 0.0 reduce-scatter.4.cloned.1.call-update
  201.1 0.0 reduce-scatter.6.cloned.1.call-start
  201.1 0.0 reduce-scatter.8.cloned.1.call-done
  201.2 0.7 multiply_convert_fusion.4
  201.9 0.1 collective-permute-start
  202.0 5.8 %collective-permute-done = bf16[8,1024]{1,0:T(8,128)(2,1)S(1)} collective-permute-done((bf16[8,1024]{1,0:T(8,128)(2,1)S(1)}, bf16[8,1024]{1,0:T(8,128)(2,1)S(1)}, u32[]{:S(2)}, u32[]{:S(2)}) %collective-permute-start) | collective-permute-done | bytes 16416 | tf_op jit(solution)/shard_map/ppermute | solution.py:76
  207.8 0.0 collective-permute-start.1
  207.8 5.9 %collective-permute-done.1 = bf16[8,1024]{1,0:T(8,128)(2,1)S(1)} collective-permute-done((bf16[8,1024]{1,0:T(8,128)(2,1)S(1)}, bf16[8,1024]{1,0:T(8,128)(2,1)S(1)}, u32[]{:S(2)}, u32[]{:S(2)}) %collective-permute-start.1) | collective-permute-done | bytes 16416 | tf_op jit(solution)/shard_map/ppermute | solution.py:76
  213.7 0.0 collective-permute-start.2
  213.7 5.9 %collective-permute-done.2 = bf16[8,1024]{1,0:T(8,128)(2,1)S(1)} collective-permute-done((bf16[8,1024]{1,0:T(8,128)(2,1)S(1)}, bf16[8,1024]{1,0:T(8,128)(2,1)S(1)}, u32[]{:S(2)}, u32[]{:S(2)}) %collective-permute-start.2) | collective-permute-done | bytes 16416 | tf_op jit(solution)/shard_map/ppermute | solution.py:76
  219.6 0.0 collective-permute-start.3
  219.6 5.9 %collective-permute-done.3 = bf16[8,1024]{1,0:T(8,128)(2,1)S(1)} collective-permute-done((bf16[8,1024]{1,0:T(8,128)(2,1)S(1)}, bf16[8,1024]{1,0:T(8,128)(2,1)S(1)}, u32[]{:S(2)}, u32[]{:S(2)}) %collective-permute-start.3) | collective-permute-done | bytes 16416 | tf_op jit(solution)/shard_map/ppermute | solution.py:76
  225.4 0.0 collective-permute-start.4
  225.4 5.9 %collective-permute-done.4 = bf16[8,1024]{1,0:T(8,128)(2,1)S(1)} collective-permute-done((bf16[8,1024]{1,0:T(8,128)(2,1)S(1)}, bf16[8,1024]{1,0:T(8,128)(2,1)S(1)}, u32[]{:S(2)}, u32[]{:S(2)}) %collective-permute-start.4) | collective-permute-done | bytes 16416 | tf_op jit(solution)/shard_map/ppermute | solution.py:76
  231.3 0.0 collective-permute-start.5
  231.3 5.9 %collective-permute-done.5 = bf16[8,1024]{1,0:T(8,128)(2,1)S(1)} collective-permute-done((bf16[8,1024]{1,0:T(8,128)(2,1)S(1)}, bf16[8,1024]{1,0:T(8,128)(2,1)S(1)}, u32[]{:S(2)}, u32[]{:S(2)}) %collective-permute-start.5) | collective-permute-done | bytes 16416 | tf_op jit(solution)/shard_map/ppermute | solution.py:76
  237.1 0.0 collective-permute-start.6
  237.1 5.9 %collective-permute-done.6 = bf16[8,1024]{1,0:T(8,128)(2,1)S(1)} collective-permute-done((bf16[8,1024]{1,0:T(8,128)(2,1)S(1)}, bf16[8,1024]{1,0:T(8,128)(2,1)S(1)}, u32[]{:S(2)}, u32[]{:S(2)}) %collective-permute-start.6) | collective-permute-done | bytes 16416 | tf_op jit(solution)/shard_map/ppermute | solution.py:76
  243.0 0.0 collective-permute-start.7
  243.0 5.9 %collective-permute-done.7 = bf16[8,1024]{1,0:T(8,128)(2,1)S(1)} collective-permute-done((bf16[8,1024]{1,0:T(8,128)(2,1)S(1)}, bf16[8,1024]{1,0:T(8,128)(2,1)S(1)}, u32[]{:S(2)}, u32[]{:S(2)}) %collective-permute-start.7) | collective-permute-done | bytes 16416 | tf_op jit(solution)/shard_map/ppermute | solution.py:76
  248.9 0.0 collective-permute-start.8
  248.9 5.9 %collective-permute-done.8 = bf16[8,1024]{1,0:T(8,128)(2,1)S(1)} collective-permute-done((bf16[8,1024]{1,0:T(8,128)(2,1)S(1)}, bf16[8,1024]{1,0:T(8,128)(2,1)S(1)}, u32[]{:S(2)}, u32[]{:S(2)}) %collective-permute-start.8) | collective-permute-done | bytes 16416 | tf_op jit(solution)/shard_map/ppermute | solution.py:76
  254.7 0.0 collective-permute-start.9
  254.7 5.9 %collective-permute-done.9 = bf16[8,1024]{1,0:T(8,128)(2,1)S(1)} collective-permute-done((bf16[8,1024]{1,0:T(8,128)(2,1)S(1)}, bf16[8,1024]{1,0:T(8,128)(2,1)S(1)}, u32[]{:S(2)}, u32[]{:S(2)}) %collective-permute-start.9) | collective-permute-done | bytes 16416 | tf_op jit(solution)/shard_map/ppermute | solution.py:76
  260.6 0.0 collective-permute-start.10
  260.6 5.9 %collective-permute-done.10 = bf16[8,1024]{1,0:T(8,128)(2,1)S(1)} collective-permute-done((bf16[8,1024]{1,0:T(8,128)(2,1)S(1)}, bf16[8,1024]{1,0:T(8,128)(2,1)S(1)}, u32[]{:S(2)}, u32[]{:S(2)}) %collective-permute-start.10) | collective-permute-done | bytes 16416 | tf_op jit(solution)/shard_map/ppermute | solution.py:76
  266.5 0.0 collective-permute-start.11
  266.5 5.9 %collective-permute-done.11 = bf16[8,1024]{1,0:T(8,128)(2,1)S(1)} collective-permute-done((bf16[8,1024]{1,0:T(8,128)(2,1)S(1)}, bf16[8,1024]{1,0:T(8,128)(2,1)S(1)}, u32[]{:S(2)}, u32[]{:S(2)}) %collective-permute-start.11) | collective-permute-done | bytes 16416 | tf_op jit(solution)/shard_map/ppermute | solution.py:76
  272.3 0.0 collective-permute-start.12
  272.3 5.9 %collective-permute-done.12 = bf16[8,1024]{1,0:T(8,128)(2,1)S(1)} collective-permute-done((bf16[8,1024]{1,0:T(8,128)(2,1)S(1)}, bf16[8,1024]{1,0:T(8,128)(2,1)S(1)}, u32[]{:S(2)}, u32[]{:S(2)}) %collective-permute-start.12) | collective-permute-done | bytes 16416 | tf_op jit(solution)/shard_map/ppermute | solution.py:76
  278.2 5.9 %collective-permute-done.13 = bf16[8,1024]{1,0:T(8,128)(2,1)S(1)} collective-permute-done((bf16[8,1024]{1,0:T(8,128)(2,1)S(1)}, bf16[8,1024]{1,0:T(8,128)(2,1)S(1)}, u32[]{:S(2)}, u32[]{:S(2)}) %collective-permute-start.13) | collective-permute-done | bytes 16416 | tf_op jit(solution)/shard_map/ppermute | solution.py:76
  284.0 0.0 collective-permute-start.14
  284.1 0.6 copy.10
  284.7 5.2 %collective-permute-done.14 = bf16[8,1024]{1,0:T(8,128)(2,1)S(1)} collective-permute-done((bf16[8,1024]{1,0:T(8,128)(2,1)S(1)}, bf16[8,1024]{1,0:T(8,128)(2,1)S(1)}, u32[]{:S(2)}, u32[]{:S(2)}) %collective-permute-start.14) | collective-permute-done | bytes 16416 | tf_op jit(solution)/shard_map/ppermute | solution.py:76
  290.0 0.0 reduce-scatter.4.cloned.1.call-done
  290.1 0.0 reduce-scatter.6.cloned.1.call-update
  290.3 1.3 convolution_bitcast_fusion
  291.6 55.4 %reduce-scatter.6.cloned.1.call-done = bf16[64,768]{1,0:T(8,128)(2,1)} async-done(((bf16[1024,768]{1,0:T(8,128)(2,1)}), bf16[64,768]{1,0:T(8,128)(2,1)}) %reduce-scatter.6.cloned.1.call-update) | async-done | bytes 98320 | tf_op jit(solution)/shard_map/reduce_scatter | solution.py:62
  347.0 1.6 convert_element_type.69
  (44 shorter events, 0.2 us)
Async XLA Ops:
  7.2 5.6 %copy-start = (bf16[128,2048]{1,0:T(8,128)(2,1)S(1)}, bf16[128,2048]{1,0:T(8,128)(2,1)}, u32[]{:S(2)}) copy-start(bf16[128,2048]{1,0:T(8,128)(2,1)} %param.10) | copy-start | bytes 1572868
  7.2 74.2 %all-gather.2.cloned.1.call-start = ((), (), s32[]{:S(2)}) async-start(), calls=%async_computation.3 | async-start | bytes 4718592 | tf_op jit(solution)/shard_map/all_gather | solution.py:33
  7.9 193.2 %reduce-scatter.8.cloned.1.call-start = ((), (), s32[]{:S(2)}) async-start(), calls=%async_computation.6 | async-start | bytes 49152 | tf_op jit(solution)/shard_map/reduce_scatter | solution.py:69
  52.0 29.3 %copy-start.3 = (s32[4096]{0:T(1024)S(1)}, s32[4096]{0:T(1024)}, u32[]{:S(2)}) copy-start(s32[4096]{0:T(1024)} %param.8) | copy-start | bytes 49156
  144.4 11.5 %copy-start.1 = (f32[500,2048]{1,0:T(8,128)S(1)}, f32[500,2048]{1,0:T(8,128)}, u32[]{:S(2)}) copy-start(f32[500,2048]{1,0:T(8,128)} %convert_element_type.57) | copy-start | bytes 12288004
  180.5 20.7 %copy-start.2 = (f32[8,2048]{1,0:T(8,128)S(1)}, f32[8,2048]{1,0:T(8,128)}, u32[]{:S(2)}) copy-start(f32[8,2048]{1,0:T(8,128)} %get-tuple-element.8) | copy-start | bytes 196612
  180.5 109.8 %copy-start.4 = (s32[128]{0:T(128)S(1)}, s32[128]{0:T(128)}, u32[]{:S(2)}) copy-start(s32[128]{0:T(128)} %param.9) | copy-start | bytes 1540
  180.5 109.6 %reduce-scatter.4.cloned.1.call-start = ((), (), s32[]{:S(2)}) async-start(), calls=%async_computation.4 | async-start | bytes 4718592 | tf_op jit(solution)/shard_map/reduce_scatter | solution.py:54
  201.1 145.9 %reduce-scatter.6.cloned.1.call-start = ((), (), s32[]{:S(2)}) async-start(), calls=%async_computation.5 | async-start | bytes 1671168 | tf_op jit(solution)/shard_map/reduce_scatter | solution.py:62
  201.9 5.9 %collective-permute-start = (bf16[8,1024]{1,0:T(8,128)(2,1)S(1)}, bf16[8,1024]{1,0:T(8,128)(2,1)S(1)}, u32[]{:S(2)}, u32[]{:S(2)}) collective-permute-start(bf16[8,1024]{1,0:T(8,128)(2,1)S(1)} %multiply_convert_fusion.4), channel_id=1, source_target_pairs={{0,1},{1,2},{2,3},{3,4},{4,5},{5,6},{6,7},{7,8},{8,9},{9,10},{10,1... | collective-permute-start | bytes 49160 | tf_op jit(solution)/shard_map/ppermute | solution.py:76
  207.8 5.9 %collective-permute-start.1 = (bf16[8,1024]{1,0:T(8,128)(2,1)S(1)}, bf16[8,1024]{1,0:T(8,128)(2,1)S(1)}, u32[]{:S(2)}, u32[]{:S(2)}) collective-permute-start(bf16[8,1024]{1,0:T(8,128)(2,1)S(1)} %collective-permute-done), channel_id=1, source_target_pairs={{0,1},{1,2},{2,3},{3,4},{4,5},{5,6},{6,7},{7,8},{8,9},{9,10},{10,1... | collective-permute-start | bytes 49160 | tf_op jit(solution)/shard_map/ppermute | solution.py:76
  213.7 5.9 %collective-permute-start.2 = (bf16[8,1024]{1,0:T(8,128)(2,1)S(1)}, bf16[8,1024]{1,0:T(8,128)(2,1)S(1)}, u32[]{:S(2)}, u32[]{:S(2)}) collective-permute-start(bf16[8,1024]{1,0:T(8,128)(2,1)S(1)} %collective-permute-done.1), channel_id=1, source_target_pairs={{0,1},{1,2},{2,3},{3,4},{4,5},{5,6},{6,7},{7,8},{8,9},{9,10},{10,1... | collective-permute-start | bytes 49160 | tf_op jit(solution)/shard_map/ppermute | solution.py:76
  219.6 5.9 %collective-permute-start.3 = (bf16[8,1024]{1,0:T(8,128)(2,1)S(1)}, bf16[8,1024]{1,0:T(8,128)(2,1)S(1)}, u32[]{:S(2)}, u32[]{:S(2)}) collective-permute-start(bf16[8,1024]{1,0:T(8,128)(2,1)S(1)} %collective-permute-done.2), channel_id=1, source_target_pairs={{0,1},{1,2},{2,3},{3,4},{4,5},{5,6},{6,7},{7,8},{8,9},{9,10},{10,1... | collective-permute-start | bytes 49160 | tf_op jit(solution)/shard_map/ppermute | solution.py:76
  225.4 5.9 %collective-permute-start.4 = (bf16[8,1024]{1,0:T(8,128)(2,1)S(1)}, bf16[8,1024]{1,0:T(8,128)(2,1)S(1)}, u32[]{:S(2)}, u32[]{:S(2)}) collective-permute-start(bf16[8,1024]{1,0:T(8,128)(2,1)S(1)} %collective-permute-done.3), channel_id=1, source_target_pairs={{0,1},{1,2},{2,3},{3,4},{4,5},{5,6},{6,7},{7,8},{8,9},{9,10},{10,1... | collective-permute-start | bytes 49160 | tf_op jit(solution)/shard_map/ppermute | solution.py:76
  231.3 5.9 %collective-permute-start.5 = (bf16[8,1024]{1,0:T(8,128)(2,1)S(1)}, bf16[8,1024]{1,0:T(8,128)(2,1)S(1)}, u32[]{:S(2)}, u32[]{:S(2)}) collective-permute-start(bf16[8,1024]{1,0:T(8,128)(2,1)S(1)} %collective-permute-done.4), channel_id=1, source_target_pairs={{0,1},{1,2},{2,3},{3,4},{4,5},{5,6},{6,7},{7,8},{8,9},{9,10},{10,1... | collective-permute-start | bytes 49160 | tf_op jit(solution)/shard_map/ppermute | solution.py:76
  237.1 5.9 %collective-permute-start.6 = (bf16[8,1024]{1,0:T(8,128)(2,1)S(1)}, bf16[8,1024]{1,0:T(8,128)(2,1)S(1)}, u32[]{:S(2)}, u32[]{:S(2)}) collective-permute-start(bf16[8,1024]{1,0:T(8,128)(2,1)S(1)} %collective-permute-done.5), channel_id=1, source_target_pairs={{0,1},{1,2},{2,3},{3,4},{4,5},{5,6},{6,7},{7,8},{8,9},{9,10},{10,1... | collective-permute-start | bytes 49160 | tf_op jit(solution)/shard_map/ppermute | solution.py:76
  243.0 5.9 %collective-permute-start.7 = (bf16[8,1024]{1,0:T(8,128)(2,1)S(1)}, bf16[8,1024]{1,0:T(8,128)(2,1)S(1)}, u32[]{:S(2)}, u32[]{:S(2)}) collective-permute-start(bf16[8,1024]{1,0:T(8,128)(2,1)S(1)} %collective-permute-done.6), channel_id=1, source_target_pairs={{0,1},{1,2},{2,3},{3,4},{4,5},{5,6},{6,7},{7,8},{8,9},{9,10},{10,1... | collective-permute-start | bytes 49160 | tf_op jit(solution)/shard_map/ppermute | solution.py:76
  248.9 5.9 %collective-permute-start.8 = (bf16[8,1024]{1,0:T(8,128)(2,1)S(1)}, bf16[8,1024]{1,0:T(8,128)(2,1)S(1)}, u32[]{:S(2)}, u32[]{:S(2)}) collective-permute-start(bf16[8,1024]{1,0:T(8,128)(2,1)S(1)} %collective-permute-done.7), channel_id=1, source_target_pairs={{0,1},{1,2},{2,3},{3,4},{4,5},{5,6},{6,7},{7,8},{8,9},{9,10},{10,1... | collective-permute-start | bytes 49160 | tf_op jit(solution)/shard_map/ppermute | solution.py:76
  254.7 5.9 %collective-permute-start.9 = (bf16[8,1024]{1,0:T(8,128)(2,1)S(1)}, bf16[8,1024]{1,0:T(8,128)(2,1)S(1)}, u32[]{:S(2)}, u32[]{:S(2)}) collective-permute-start(bf16[8,1024]{1,0:T(8,128)(2,1)S(1)} %collective-permute-done.8), channel_id=1, source_target_pairs={{0,1},{1,2},{2,3},{3,4},{4,5},{5,6},{6,7},{7,8},{8,9},{9,10},{10,1... | collective-permute-start | bytes 49160 | tf_op jit(solution)/shard_map/ppermute | solution.py:76
  260.6 5.9 %collective-permute-start.10 = (bf16[8,1024]{1,0:T(8,128)(2,1)S(1)}, bf16[8,1024]{1,0:T(8,128)(2,1)S(1)}, u32[]{:S(2)}, u32[]{:S(2)}) collective-permute-start(bf16[8,1024]{1,0:T(8,128)(2,1)S(1)} %collective-permute-done.9), channel_id=1, source_target_pairs={{0,1},{1,2},{2,3},{3,4},{4,5},{5,6},{6,7},{7,8},{8,9},{9,10},{10,1... | collective-permute-start | bytes 49160 | tf_op jit(solution)/shard_map/ppermute | solution.py:76
  266.5 5.9 %collective-permute-start.11 = (bf16[8,1024]{1,0:T(8,128)(2,1)S(1)}, bf16[8,1024]{1,0:T(8,128)(2,1)S(1)}, u32[]{:S(2)}, u32[]{:S(2)}) collective-permute-start(bf16[8,1024]{1,0:T(8,128)(2,1)S(1)} %collective-permute-done.10), channel_id=1, source_target_pairs={{0,1},{1,2},{2,3},{3,4},{4,5},{5,6},{6,7},{7,8},{8,9},{9,10},{10,1... | collective-permute-start | bytes 49160 | tf_op jit(solution)/shard_map/ppermute | solution.py:76
  272.3 5.9 %collective-permute-start.12 = (bf16[8,1024]{1,0:T(8,128)(2,1)S(1)}, bf16[8,1024]{1,0:T(8,128)(2,1)S(1)}, u32[]{:S(2)}, u32[]{:S(2)}) collective-permute-start(bf16[8,1024]{1,0:T(8,128)(2,1)S(1)} %collective-permute-done.11), channel_id=1, source_target_pairs={{0,1},{1,2},{2,3},{3,4},{4,5},{5,6},{6,7},{7,8},{8,9},{9,10},{10,1... | collective-permute-start | bytes 49160 | tf_op jit(solution)/shard_map/ppermute | solution.py:76
  278.2 5.9 %collective-permute-start.13 = (bf16[8,1024]{1,0:T(8,128)(2,1)S(1)}, bf16[8,1024]{1,0:T(8,128)(2,1)S(1)}, u32[]{:S(2)}, u32[]{:S(2)}) collective-permute-start(bf16[8,1024]{1,0:T(8,128)(2,1)S(1)} %collective-permute-done.12), channel_id=1, source_target_pairs={{0,1},{1,2},{2,3},{3,4},{4,5},{5,6},{6,7},{7,8},{8,9},{9,10},{10,1... | collective-permute-start | bytes 49160 | tf_op jit(solution)/shard_map/ppermute | solution.py:76
  284.0 5.9 %collective-permute-start.14 = (bf16[8,1024]{1,0:T(8,128)(2,1)S(1)}, bf16[8,1024]{1,0:T(8,128)(2,1)S(1)}, u32[]{:S(2)}, u32[]{:S(2)}) collective-permute-start(bf16[8,1024]{1,0:T(8,128)(2,1)S(1)} %collective-permute-done.13), channel_id=1, source_target_pairs={{0,1},{1,2},{2,3},{3,4},{4,5},{5,6},{6,7},{7,8},{8,9},{9,10},{10,1... | collective-permute-start | bytes 49160 | tf_op jit(solution)/shard_map/ppermute | solution.py:76
Sparse Core Ops, SparseCore 0:
  9.5 47.6 all-gather.1
  180.6 7.2 reduce-scatter.7
  201.2 40.7 reduce-scatter.3
  290.2 56.7 reduce-scatter.5
